TPU v7x, 128 devices: a whole 4x4x4 slice. The times are simulated.
128 devices in a mesh: section: 8 (over z, core), rows: 16 (over y, x).
Axes of the slice: x: 4, y: 4, z: 4, core: 2. Of those that a mesh axis runs over, the one named last changes fastest.
Arguments:
- features: bfloat16 [2048, 1536], P('rows'), may hold values from -6 to 6
- ages: int32 [2048], P('rows'), may hold values from 0 to 15
- age_table: bfloat16 [16, 1536], replicated, may hold values from -3 to 3
- returns: float32 [2048], P('rows'), may hold values from -6 to 6
- owners: int32 [2048, 1], P('rows'), may hold values from 0 to 15; in each aligned block of 128 rows (0 to 127, 128 to 255, ...) at most 32 rows name the same one
- slots: int32 [2048], P('rows'), may hold values from 0 to 4095
- norm_gain: float32 [8, 1536], P('section'), may hold values from 0.1 to 1.9
- w_gate: bfloat16 [8, 1536, 8960], P('section', None, 'rows'), may hold values from -0.15625 to 0.15625
- w_up: bfloat16 [8, 1536, 8960], P('section', None, 'rows'), may hold values from -0.15625 to 0.15625
- w_down: bfloat16 [8, 8960, 1536], P('section', 'rows'), may hold values from -0.0625 to 0.0625
- final_gain: float32 [1536], replicated, may hold values from 0.1 to 1.9
- reward_head: float32 [1536], replicated, may hold values from -0.15625 to 0.15625
- old_priority: float32 [65536], P('rows'), may hold values from 0.05 to 2
Outputs:
- rewards: float32 [2048], P(('rows', 'section'))
- weights: float32 [65536], P(('rows', 'section'))
Inputs may be any that keep to these rules, and one draw needn't show every extreme that they name: `owners`: among the rows of one device at most 32 name the same owner; in every draw some owner is named by exactly 32 rows of some device.
All inputs are finite; a program needn't handle non-finite values.
Results may differ from a plain program's by a relative error of at most 0.04.
Values may be sent and summed in bfloat16 or wider, within the bound.
A program may use at most 64 MiB of HBM per device.

v0:
```python
import functools

import jax
import jax.numpy as jnp
from jax import lax
from jax.experimental import pallas as pl
from jax.experimental.pallas import tpu as pltpu
from jax.sharding import PartitionSpec as P

MICRO = 8
MESH = pl.DeviceIdType.MESH
LANES = 128


def chunks(total, size):
    return [(at, min(size, total - at)) for at in range(0, total, size)]


def flipped(index, mask):
    moved, bit = index, 1
    while bit <= mask:
        if mask & bit:
            moved = moved + bit * (1 - 2 * lax.rem(index // bit, 2))
        bit *= 2
    return moved


def remote(src, dst, send_sem, recv_sem, where):
    return pltpu.make_async_remote_copy(
        src_ref=src, dst_ref=dst, send_sem=send_sem, recv_sem=recv_sem,
        device_id=where, device_id_type=MESH,
    )


def kernel(
    sections, groups,
    features, ages, age_table, returns, owners, slots, gain, w_gate, w_up, w_down,
    final_gain, head, old,
    rewards_out, weights_out,
    wg, wu, wd, wg_up, wu_up, x_in, x_out, gathered, hidden, part, part_in, paired, paired_in,
    final_row, reward_cols, marks, marks_wide, result, prio_wide, refreshed, sums,
    w_sem,
    ag_send, ag_recv, fw_send, fw_recv, pr_send, pr_recv, rs_send, rs_recv, z_send, z_recv,
    mk_send, mk_recv, up_send, up_recv, rw_send, rw_recv, sm_send, sm_recv,
):
    sec = lax.axis_index("section")
    me = lax.axis_index("rows")
    chips = groups // 2
    chip, core = me // 2, lax.rem(me, 2)
    other = 1 - core
    sibling = chip * 2 + other
    far_first = sorted(range(1, chips), key=lambda j: (-j.bit_count(), j))
    block, width = x_in.shape[1], x_in.shape[2]
    rows = x_in.shape[0] * block
    ff = hidden.shape[1]
    last = sections - 1

    loads = [
        pltpu.make_async_copy(w_gate, wg, w_sem.at[0]),
        pltpu.make_async_copy(w_up, wu, w_sem.at[1]),
        pltpu.make_async_copy(w_down, wd, w_sem.at[2]),
    ]
    loads[0].start()
    loads[1].start()

    barrier = pltpu.get_barrier_semaphore()
    for j in range(1, groups):
        pl.semaphore_signal(barrier, inc=1, device_id={"rows": lax.rem(me + j, groups)}, device_id_type=MESH)
    for j in range(1, sections):
        pl.semaphore_signal(barrier, inc=1, device_id={"section": lax.rem(sec + j, sections)}, device_id_type=MESH)

    marks[me] = (owners[...] * (old.shape[0] * LANES) + slots[...]).astype(jnp.float32)

    for i in range(final_gain.shape[0]):
        final_row[0:1, i * LANES:(i + 1) * LANES] = final_gain[i:i + 1, :]
        final_row[1:2, i * LANES:(i + 1) * LANES] = head[i:i + 1, :]

    @pl.when(sec == 0)
    def _():
        tall = jnp.transpose(jnp.broadcast_to(ages[...].astype(jnp.float32), (LANES, rows)))
        buckets = age_table.shape[0]
        onehot = (
            tall[:, :buckets] == lax.broadcasted_iota(jnp.int32, (rows, buckets), 1).astype(jnp.float32)
        ).astype(jnp.float32).astype(jnp.bfloat16)
        for at, size in chunks(width, 512):
            entry = features[:, at:at + size].astype(jnp.float32) + jnp.dot(
                onehot, age_table[:, at:at + size], preferred_element_type=jnp.float32
            )
            x_in[:, :, at:at + size] = entry.astype(jnp.bfloat16).reshape(MICRO, block, size)

    pl.semaphore_wait(barrier, groups - 1 + sections - 1)

    def to_group(ref, send, recv, j):
        return remote(ref.at[me], ref.at[me], send.at[j], recv.at[j], {"rows": lax.rem(me + j, groups)})

    def from_group(ref, send, recv, j):
        spot = ref.at[lax.rem(me + groups - j, groups)]
        return remote(spot, spot, send.at[j], recv.at[j], {"rows": lax.rem(me + j, groups)})

    def peer(j):
        return {"rows": flipped(chip, j) * 2 + core}

    def ag_copy(m, j, spot):
        block_ref = gathered.at[m, core, spot]
        return remote(block_ref, block_ref, ag_send.at[m, j - 1], ag_recv.at[m, j - 1], peer(j))

    def fw_copy(m, half):
        half_ref = gathered.at[m, half]
        return remote(half_ref, half_ref, fw_send.at[m], fw_recv.at[m], {"rows": sibling})

    def pr_copy(m):
        return remote(part.at[m, other], part_in.at[m], pr_send.at[m], pr_recv.at[m], {"rows": sibling})

    def rs_copy(m, j):
        return remote(
            paired.at[m, flipped(chip, j)], paired_in.at[m, j - 1],
            rs_send.at[m, j - 1], rs_recv.at[m, j - 1], peer(j),
        )

    def z_copy(m):
        return remote(x_out.at[m], x_in.at[m], z_send.at[m], z_recv.at[m], {"section": jnp.minimum(sec + 1, last)})

    def z_back(m):
        return remote(x_out.at[m], x_in.at[m], z_send.at[m], z_recv.at[m], {"section": jnp.maximum(sec - 1, 0)})

    def stage_a(m):
        @pl.when(sec > 0)
        def _():
            z_back(m).wait_recv()

        wide = x_in[m].astype(jnp.float32)
        scale = lax.rsqrt(jnp.mean(wide * wide, axis=-1, keepdims=True) + 1e-06)
        gathered[m, core, chip] = (wide * scale * gain[...]).astype(jnp.bfloat16)
        for j in far_first:
            ag_copy(m, j, chip).start()

    def stage_f(m):
        for j in far_first:
            ag_copy(m, j, flipped(chip, j)).wait_recv()
        fw_copy(m, core).start()

    def stage_b(m):
        fw_copy(m, other).wait_recv()
        piece = gathered[m].reshape(groups * block, width)
        for at, size in chunks(ff, 256):
            gate = jnp.dot(piece, wg_up[:, at:at + size], preferred_element_type=jnp.float32)
            upper = jnp.dot(piece, wu_up[:, at:at + size], preferred_element_type=jnp.float32)
            hidden[:, at:at + size] = (gate / (1.0 + jnp.exp(-gate)) * upper).astype(jnp.bfloat16)
        units = hidden[...]
        for at, size in chunks(width, 256):
            down = jnp.dot(units, wd[:, at:at + size], preferred_element_type=jnp.float32)
            part[m, :, :, :, at:at + size] = down.astype(jnp.bfloat16).reshape(2, chips, block, size)
        pr_copy(m).start()

    def stage_r(m):
        pr_copy(m).wait_recv()
        both = part[m, core].astype(jnp.float32) + part_in[m].astype(jnp.float32)
        paired[m] = both.astype(jnp.bfloat16)
        for j in far_first:
            rs_copy(m, j).start()

    def stage_c(m):
        total = x_in[m].astype(jnp.float32) + paired[m, chip].astype(jnp.float32)
        for j in far_first:
            rs_copy(m, j).wait_recv()
            total = total + paired_in[m, j - 1].astype(jnp.float32)
        state = total.astype(jnp.bfloat16)
        x_out[m] = state

        @pl.when(sec < last)
        def _():
            z_copy(m).start()

        @pl.when(sec == last)
        def _():
            wide = state.astype(jnp.float32)
            scale = lax.rsqrt(jnp.mean(wide * wide, axis=-1, keepdims=True) + 1e-06)
            value = jnp.sum(wide * scale * final_row[0:1] * final_row[1:2], axis=-1, keepdims=True)
            reward_cols[m] = jnp.broadcast_to(value, (block, LANES))

    stage_a(0)
    for j in range(1, groups):
        to_group(marks, mk_send, mk_recv, j).start()
    for load, flat, tall in ((loads[0], wg, wg_up), (loads[1], wu, wu_up)):
        load.wait()
        if load is loads[0]:
            loads[2].start()
        for at, size in chunks(ff, 256):
            tall[:, at:at + size] = jnp.transpose(flat[at:at + size, :])
    stage_f(0)
    loads[2].wait()

    def step(t, carry):
        @pl.when(t + 1 < MICRO)
        def _():
            stage_a(t + 1)

        @pl.when(t < MICRO)
        def _():
            stage_b(t)

        @pl.when(t >= 1)
        def _():
            stage_c(t - 1)

        @pl.when(t < MICRO)
        def _():
            stage_r(t)

        @pl.when(t + 1 < MICRO)
        def _():
            stage_f(t + 1)

        return carry

    lax.fori_loop(0, MICRO + 1, step, 0)

    for j in range(1, groups):
        from_group(marks, mk_send, mk_recv, j).wait_recv()
    for r in range(groups):
        marks_wide[r] = jnp.transpose(jnp.broadcast_to(marks[r], (LANES, rows)))

    def up_copy(j):
        return remote(result.at[me], result.at[me], up_send.at[j - 1], up_recv.at[0], {"section": last - j})

    @pl.when(sec == last)
    def _():
        square = reward_cols[...].reshape(rows, LANES)
        on_line = lax.broadcasted_iota(jnp.int32, (rows, rows), 0) == lax.broadcasted_iota(jnp.int32, (rows, rows), 1)
        row = jnp.sum(jnp.where(on_line, square, 0.0), axis=0, keepdims=True)
        priority = jnp.exp(0.6 * jnp.log(jnp.abs(row - returns[...]) + 0.05))
        result[me, 0:1] = row
        result[me, 1:2] = priority
        for j in range(1, sections):
            up_copy(j).start()

    @pl.when(sec < last)
    def _():
        up_copy(1).wait_recv()

    for j in range(1, groups):
        to_group(result, rw_send, rw_recv, j).start()

    mine = result[me, 0:1]
    share = rows // sections
    picked = mine[:, 0:share]
    for s in range(1, sections):
        picked = jnp.where(sec == s, mine[:, s * share:(s + 1) * share], picked)
    rewards_out[...] = picked

    for j in range(1, groups):
        from_group(result, rw_send, rw_recv, j).wait_recv()
    for r in range(groups):
        prio_wide[r] = jnp.transpose(jnp.broadcast_to(result[r, 1:2], (LANES, rows)))

    lines = old.shape[0]
    table = lines * LANES
    batch = 4
    lane = lax.broadcasted_iota(jnp.int32, (1, LANES), 1).astype(jnp.float32)

    def match(g, carry):
        first = (me * table + g * (batch * LANES)).astype(jnp.float32)
        names = [first + (q * LANES) + lane for q in range(batch)]

        def one(r, best):
            best = list(best)
            for i in range(0, rows, 8):
                mark = marks_wide[r, i:i + 8, :]
                prio = prio_wide[r, i:i + 8, :]
                for q in range(batch):
                    best[q] = jnp.maximum(best[q], jnp.where(mark == names[q], prio, 0.0))
            return tuple(best)

        best = lax.fori_loop(0, groups, one, tuple(jnp.zeros((8, LANES), jnp.float32) for _ in range(batch)))
        for q in range(batch):
            top = jnp.max(best[q], axis=0, keepdims=True)
            at = pl.ds(g * batch + q, 1)
            refreshed[at, :] = jnp.where(top > 0.0, top, old[at, :])
        return carry

    lax.fori_loop(0, lines // batch, match, 0)
    subtotal = jnp.sum(jnp.sum(refreshed[...], axis=0, keepdims=True), axis=1, keepdims=True)
    sums[me] = jnp.broadcast_to(subtotal, (1, LANES))
    for j in range(1, groups):
        to_group(sums, sm_send, sm_recv, j).start()

    for m in range(MICRO):
        for j in far_first:
            ag_copy(m, j, chip).wait_send()
            rs_copy(m, j).wait_send()
        fw_copy(m, core).wait_send()
        pr_copy(m).wait_send()

    @pl.when(sec < last)
    def _():
        for m in range(MICRO):
            z_copy(m).wait_send()

    @pl.when(sec == last)
    def _():
        for j in range(1, sections):
            up_copy(j).wait_send()

    for j in range(1, groups):
        to_group(marks, mk_send, mk_recv, j).wait_send()
        to_group(result, rw_send, rw_recv, j).wait_send()

    for j in range(1, groups):
        from_group(sums, sm_send, sm_recv, j).wait_recv()
    total = sums[0]
    for r in range(1, groups):
        total = total + sums[r]
    tall = lines // sections
    weights_out[...] = refreshed[pl.ds(sec * tall, tall), :] * (table * groups / total)
    for j in range(1, groups):
        to_group(sums, sm_send, sm_recv, j).wait_send()


def handed(rewards, weights, rewards_out, weights_out):
    rewards_out[...] = rewards[...]
    weights_out[...] = weights[...]


def on_device(
    features, ages, age_table, returns, owners, slots, norm_gain,
    w_gate, w_up, w_down, final_gain, reward_head, old_priority,
):
    sections, groups = lax.axis_size("section"), lax.axis_size("rows")
    rows, width = features.shape
    block = rows // MICRO
    chips = groups // 2
    ff = w_gate.shape[2]
    table = old_priority.shape[0]
    lines = table // LANES
    vmem = pl.BlockSpec(memory_space=pltpu.VMEM)
    far = pl.BlockSpec(memory_space=pl.ANY)
    bf16, f32, dma = jnp.bfloat16, jnp.float32, pltpu.SemaphoreType.DMA
    rewards, weights = pl.pallas_call(
        functools.partial(kernel, sections, groups),
        out_shape=(
            jax.ShapeDtypeStruct((1, rows // sections), f32),
            jax.ShapeDtypeStruct((lines // sections, LANES), f32),
        ),
        in_specs=[vmem] * 7 + [far] * 3 + [vmem] * 3,
        out_specs=(vmem, vmem),
        scratch_shapes=[
            pltpu.VMEM((ff, width), bf16),
            pltpu.VMEM((ff, width), bf16),
            pltpu.VMEM((ff, width), bf16),
            pltpu.VMEM((width, ff), bf16),
            pltpu.VMEM((width, ff), bf16),
            pltpu.VMEM((MICRO, block, width), bf16),
            pltpu.VMEM((MICRO, block, width), bf16),
            pltpu.VMEM((MICRO, 2, chips, block, width), bf16),
            pltpu.VMEM((groups * block, ff), bf16),
            pltpu.VMEM((MICRO, 2, chips, block, width), bf16),
            pltpu.VMEM((MICRO, chips, block, width), bf16),
            pltpu.VMEM((MICRO, chips, block, width), bf16),
            pltpu.VMEM((MICRO, chips - 1, block, width), bf16),
            pltpu.VMEM((2, width), f32),
            pltpu.VMEM((MICRO, block, LANES), f32),
            pltpu.VMEM((groups, 1, rows), f32),
            pltpu.VMEM((groups, rows, LANES), f32),
            pltpu.VMEM((groups, 2, rows), f32),
            pltpu.VMEM((groups, rows, LANES), f32),
            pltpu.VMEM((lines, LANES), f32),
            pltpu.VMEM((groups, 1, LANES), f32),
            dma((3,)),
            dma((MICRO, chips - 1)), dma((MICRO, chips - 1)),
            dma((MICRO,)), dma((MICRO,)),
            dma((MICRO,)), dma((MICRO,)),
            dma((MICRO, chips - 1)), dma((MICRO, chips - 1)),
            dma((MICRO,)), dma((MICRO,)),
            dma((groups,)), dma((groups,)),
            dma((sections - 1,)), dma((1,)),
            dma((groups,)), dma((groups,)),
            dma((groups,)), dma((groups,)),
        ],
        compiler_params=pltpu.CompilerParams(
            collective_id=0, has_side_effects=True, vmem_limit_bytes=56 * 1024 * 1024
        ),
        name="refresh",
    )(
        features, ages.reshape(1, rows), age_table, returns.reshape(1, rows),
        owners.reshape(1, rows), slots.reshape(1, rows),
        norm_gain, w_gate[0].T, w_up[0].T, w_down[0],
        final_gain.reshape(-1, LANES), reward_head.reshape(-1, LANES),
        old_priority.reshape(lines, LANES),
    )
    rewards, weights = pl.pallas_call(
        handed, out_shape=tuple(jax.ShapeDtypeStruct(each.shape, f32) for each in (rewards, weights)),
        in_specs=[vmem, vmem], out_specs=(vmem, vmem), name="handed",
    )(rewards, weights)
    return rewards.reshape(-1), weights.reshape(-1)


def solution(mesh):
    placed = (
        P("rows", None),
        P("rows"),
        P(),
        P("rows"),
        P("rows", None),
        P("rows"),
        P("section", None),
        P("section", None, "rows"),
        P("section", None, "rows"),
        P("section", "rows", None),
        P(),
        P(),
        P("rows"),
    )
    return jax.shard_map(
        on_device,
        mesh=mesh,
        in_specs=placed,
        out_specs=(P(("rows", "section")), P(("rows", "section"))),
        check_vma=False,
    )
```

profile of v0, /device:TPU:1, one launch (start us, length us, event | category | flops | bytes accessed | tf_op | source)
XLA Modules:
  0.0 615.7 jit_solution(11876926430390465915)
XLA Ops:
  0.6 613.8 %refresh.1 = (f32[1,16]{1,0:T(1,128)}, f32[4,128]{1,0:T(4,128)}) custom-call(bf16[128,1536]{1,0:T(8,128)(2,1)} %features.1, s32[1,128]{1,0:T(1,128)} %bitcast.22, bf16[16,1536]{1,0:T(8,128)(2,1)} %age_table.1, f32[1,128]{1,0:T(1,128)} %bitcast.23, s32[1,128]{1,0:T(1,128)} %bitcast.24, s32[1,128]{1,0:T(1,128)} %bitcast.25, f32[1,1536]{1,0:T(1,128)} %gain.1, ...), custom_call_target="tpu_custom_call" | custom-call | tf_op jit(solution)/shard_map/refresh/pallas_call | solution.py:338
  614.4 1.3 handed.1
where the time goes:
time: 617 us; the launch traced here: 616 us
  Pallas kernels  615 us (100%)
    pallas_call x1, Pallas kernels, on_device(): pl.pallas_call(functools.partial(kernel, sections, groups), out_shape=(ja...  614 us

commit v1 on v0

v1 whole, which is shorter than its diff:
```python
import functools

import jax
import jax.numpy as jnp
from jax import lax
from jax.experimental import pallas as pl
from jax.experimental.pallas import tpu as pltpu
from jax.sharding import PartitionSpec as P

MICRO = 16
SIDE = 4
MESH = pl.DeviceIdType.MESH
LANES = 128


def chunks(total, size):
    return [(at, min(size, total - at)) for at in range(0, total, size)]


def remote(src, dst, send_sem, recv_sem, where):
    return pltpu.make_async_remote_copy(
        src_ref=src, dst_ref=dst, send_sem=send_sem, recv_sem=recv_sem,
        device_id=where, device_id_type=MESH,
    )


def kernel(
    sections, groups,
    features, ages, age_table, returns, owners, slots, gain, w_gate, w_up, w_down,
    final_gain, head, old,
    rewards_out, weights_out,
    wg, wu, wd, w_both, state, gathered, hidden, part, part_in, line_out, line_in, last_in,
    final_row, reward_cols, marks, marks_wide, result, prio_wide, refreshed, sums,
    w_sem,
    in_send, ag_send, ag_recv, rs_send, rs_recv, ln_send, ln_recv, fn_recv,
    mk_send, mk_recv, up_send, up_recv, rw_send, rw_recv, sm_send, sm_recv,
):
    sec = lax.axis_index("section")
    me = lax.axis_index("rows")
    spot = (lax.rem(me, SIDE), me // SIDE)
    block, width = state.shape[2], state.shape[3]
    rows = features.shape[0]
    ff = hidden.shape[1]
    even = ff // 256 * 256
    rest = ff - even
    last = sections - 1
    rounds = MICRO // SIDE

    def step_on(axis, d):
        return lax.rem(spot[axis] + d, SIDE)

    def on_line(axis, index):
        return spot[1] * SIDE + index if axis == 0 else index * SIDE + spot[0]

    loads = [
        pltpu.make_async_copy(w_gate, wg, w_sem.at[0]),
        pltpu.make_async_copy(w_up, wu, w_sem.at[1]),
        pltpu.make_async_copy(w_down, wd, w_sem.at[2]),
    ]
    for load in loads:
        load.start()

    barrier = pltpu.get_barrier_semaphore()
    for j in range(1, groups):
        pl.semaphore_signal(barrier, inc=1, device_id={"rows": lax.rem(me + j, groups)}, device_id_type=MESH)
    for j in range(1, sections):
        pl.semaphore_signal(barrier, inc=1, device_id={"section": lax.rem(sec + j, sections)}, device_id_type=MESH)
    before = lax.rem(sec + last, sections)
    for axis in range(2):
        for d in range(1, SIDE):
            pl.semaphore_signal(
                barrier, inc=1, device_id={"section": before, "rows": on_line(axis, step_on(axis, d))}, device_id_type=MESH
            )

    marks[me] = (owners[...] * (old.shape[0] * LANES) + slots[...]).astype(jnp.float32)

    for i in range(final_gain.shape[0]):
        final_row[0:1, i * LANES:(i + 1) * LANES] = final_gain[i:i + 1, :]
        final_row[1:2, i * LANES:(i + 1) * LANES] = head[i:i + 1, :]

    @pl.when(sec == 0)
    def _():
        tall = jnp.transpose(jnp.broadcast_to(ages[...].astype(jnp.float32), (LANES, rows)))
        buckets = age_table.shape[0]
        onehot = (
            tall[:, :buckets] == lax.broadcasted_iota(jnp.int32, (rows, buckets), 1).astype(jnp.float32)
        ).astype(jnp.float32).astype(jnp.bfloat16)
        for at, size in chunks(width, 512):
            entry = features[:, at:at + size].astype(jnp.float32) + jnp.dot(
                onehot, age_table[:, at:at + size], preferred_element_type=jnp.float32
            )
            entry = entry.astype(jnp.bfloat16).reshape(2, rounds, block, size)
            for h in range(2):
                for k in range(rounds):
                    state[k * SIDE + spot[1 - h], h, :, at:at + size] = entry[h, k]

    pl.semaphore_wait(barrier, groups - 1 + sections - 1 + 2 * (SIDE - 1))

    def to_group(ref, send, recv, j):
        return remote(ref.at[me], ref.at[me], send.at[j], recv.at[j], {"rows": lax.rem(me + j, groups)})

    def from_group(ref, send, recv, j):
        spot_ref = ref.at[lax.rem(me + groups - j, groups)]
        return remote(spot_ref, spot_ref, send.at[j], recv.at[j], {"rows": lax.rem(me + j, groups)})

    def in_copy(k, h, d):
        t = k * SIDE + spot[1 - h]
        ref = state.at[t, h]
        return remote(
            ref, ref, in_send.at[k, h, d - 1], ln_recv.at[t, h, 0], {"rows": on_line(1 - h, step_on(1 - h, d))}
        )

    def in_from(t, h):
        ref = state.at[t, h]
        return remote(ref, ref, in_send.at[0, h, 0], ln_recv.at[t, h, 0], {"rows": on_line(1 - h, step_on(1 - h, 1))})

    def ag_copy(t, h, d, shard):
        ref = gathered.at[t, h, shard]
        return remote(
            ref, ref, ag_send.at[t, h, d - 1], ag_recv.at[t, h, d - 1], {"rows": on_line(h, step_on(h, d))}
        )

    def rs_copy(t, h, d):
        return remote(
            part.at[t, h, step_on(h, d)], part_in.at[t, h, d - 1], rs_send.at[t, h, d - 1], rs_recv.at[t, h, d - 1],
            {"rows": on_line(h, step_on(h, d))},
        )

    def line_copy(t, h, d):
        own = spot[1 - h]
        return remote(
            line_out.at[t, h], line_in.at[t, h, own], ln_send.at[t, h, d], ln_recv.at[t, h, own],
            {"section": jnp.minimum(sec + 1, last), "rows": on_line(1 - h, step_on(1 - h, d))},
        )

    def line_from(t, h, i):
        return remote(
            line_out.at[t, h], line_in.at[t, h, i], ln_send.at[t, h, 0], ln_recv.at[t, h, i],
            {"section": jnp.maximum(sec - 1, 0)},
        )

    def home_of(t):
        return lax.rem(t, SIDE)

    def last_copy(t, h):
        home = home_of(t)
        d = lax.rem(home + SIDE - spot[1 - h] + SIDE - 1, SIDE)
        k = t // SIDE
        return remote(
            line_out.at[t, h], last_in.at[k, h, d], ln_send.at[t, h, 0], fn_recv.at[k, h, d],
            {"rows": on_line(1 - h, home)},
        )

    def last_from(k, h, d):
        ref = last_in.at[k, h, d - 1]
        return remote(ref, ref, ln_send.at[0, h, 0], fn_recv.at[k, h, d - 1], {"rows": on_line(1 - h, step_on(1 - h, d))})

    def enter(t):
        for h in range(2):
            @pl.when(sec > 0)
            def _():
                for i in range(SIDE):
                    line_from(t, h, i).wait_recv()
                total = line_in[t, h, 0].astype(jnp.float32)
                for i in range(1, SIDE):
                    total = total + line_in[t, h, i].astype(jnp.float32)
                state[t, h] = total.astype(jnp.bfloat16)

            @pl.when((sec == 0) & (spot[1 - h] != home_of(t)))
            def _():
                in_from(t, h).wait_recv()

            wide = state[t, h].astype(jnp.float32)
            scale = lax.rsqrt(jnp.mean(wide * wide, axis=-1, keepdims=True) + 1e-06)
            gathered[t, h, spot[h]] = (wide * scale * gain[...]).astype(jnp.bfloat16)
            for d in (2, 1, 3):
                ag_copy(t, h, d, spot[h]).start()

    def work(t):
        for h in range(2):
            for d in (1, 3, 2):
                ag_copy(t, h, d, step_on(h, SIDE - d)).wait_recv()
        piece = gathered[t].reshape(2 * SIDE * block, width)
        for at in range(0, even, 256):
            gate = jnp.dot(piece, w_both[:, at:at + 256], preferred_element_type=jnp.float32)
            upper = jnp.dot(piece, w_both[:, even + at:even + at + 256], preferred_element_type=jnp.float32)
            hidden[:, at:at + 256] = (gate / (1.0 + jnp.exp(-gate)) * upper).astype(jnp.bfloat16)
        ends = jnp.dot(piece, w_both[:, 2 * even:2 * even + 256], preferred_element_type=jnp.float32)
        gate, upper = ends[:, :rest], ends[:, LANES:LANES + rest]
        hidden[:, even:ff] = (gate / (1.0 + jnp.exp(-gate)) * upper).astype(jnp.bfloat16)
        units = hidden[...]
        for at, size in chunks(width, 256):
            down = jnp.dot(units, wd[:, at:at + size], preferred_element_type=jnp.float32)
            part[t, :, :, :, at:at + size] = down.astype(jnp.bfloat16).reshape(2, SIDE, block, size)
        for h in range(2):
            for d in (2, 1, 3):
                rs_copy(t, h, d).start()

    def leave(t):
        home = home_of(t)
        for h in range(2):
            total = part[t, h, spot[h]].astype(jnp.float32)
            total = total + jnp.where(spot[1 - h] == home, state[t, h].astype(jnp.float32), 0.0)
            for d in range(1, SIDE):
                rs_copy(t, h, d).wait_recv()
                total = total + part_in[t, h, d - 1].astype(jnp.float32)
            line_out[t, h] = total.astype(jnp.bfloat16)

            @pl.when(sec < last)
            def _():
                for d in (2, 1, 3, 0):
                    line_copy(t, h, d).start()

            @pl.when((sec == last) & (spot[1 - h] != home))
            def _():
                last_copy(t, h).start()

    def finish(t):
        k = t // SIDE
        for h in range(2):
            @pl.when(spot[1 - h] == home_of(t))
            def _():
                total = line_out[t, h].astype(jnp.float32)
                for d in range(1, SIDE):
                    last_from(k, h, d).wait_recv()
                    total = total + last_in[k, h, d - 1].astype(jnp.float32)
                wide = total.astype(jnp.bfloat16).astype(jnp.float32)
                scale = lax.rsqrt(jnp.mean(wide * wide, axis=-1, keepdims=True) + 1e-06)
                value = jnp.sum(wide * scale * final_row[0:1] * final_row[1:2], axis=-1, keepdims=True)
                reward_cols[h, k] = jnp.broadcast_to(value, (block, LANES))

    @pl.when(sec == 0)
    def _():
        for k in range(rounds):
            for h in range(2):
                for d in (2, 1, 3):
                    in_copy(k, h, d).start()

    def turned(load, flat, first):
        load.wait()
        for at in range(0, even, 256):
            w_both[:, first * even + at:first * even + at + 256] = jnp.transpose(flat[at:at + 256, :])
        w_both[:, 2 * even + first * LANES:2 * even + first * LANES + rest] = jnp.transpose(flat[even:ff, :])

    w_both[:, 2 * even:2 * even + 256] = jnp.zeros((width, 256), jnp.bfloat16)
    turned(loads[0], wg, 0)
    for j in range(1, groups):
        to_group(marks, mk_send, mk_recv, j).start()

    @pl.when(sec == 0)
    def _():
        enter(0)

    turned(loads[1], wu, 1)
    loads[2].wait()

    @pl.when(sec > 0)
    def _():
        enter(0)

    def step(t, carry):
        work(t)

        @pl.when(t + 1 < MICRO)
        def _():
            enter(t + 1)

        @pl.when((sec == last) & (t > 0))
        def _():
            finish(t - 1)

        leave(t)
        return carry

    lax.fori_loop(0, MICRO, step, 0)

    for j in range(1, groups):
        from_group(marks, mk_send, mk_recv, j).wait_recv()
    for r in range(groups):
        marks_wide[r] = jnp.transpose(jnp.broadcast_to(marks[r], (LANES, rows)))

    def up_copy(j):
        return remote(result.at[me], result.at[me], up_send.at[j - 1], up_recv.at[0], {"section": last - j})

    @pl.when(sec == last)
    def _():
        finish(MICRO - 1)
        square = reward_cols[...].reshape(rows, LANES)
        on_diagonal = lax.broadcasted_iota(jnp.int32, (rows, rows), 0) == lax.broadcasted_iota(jnp.int32, (rows, rows), 1)
        row = jnp.sum(jnp.where(on_diagonal, square, 0.0), axis=0, keepdims=True)
        priority = jnp.exp(0.6 * jnp.log(jnp.abs(row - returns[...]) + 0.05))
        result[me, 0:1] = row
        result[me, 1:2] = priority
        for j in range(1, sections):
            up_copy(j).start()

    @pl.when(sec < last)
    def _():
        up_copy(1).wait_recv()

    for j in range(1, groups):
        to_group(result, rw_send, rw_recv, j).start()

    mine = result[me, 0:1]
    share = rows // sections
    picked = mine[:, 0:share]
    for s in range(1, sections):
        picked = jnp.where(sec == s, mine[:, s * share:(s + 1) * share], picked)
    rewards_out[...] = picked

    for j in range(1, groups):
        from_group(result, rw_send, rw_recv, j).wait_recv()
    for r in range(groups):
        prio_wide[r] = jnp.transpose(jnp.broadcast_to(result[r, 1:2], (LANES, rows)))

    lines = old.shape[0]
    table = lines * LANES
    batch = 4
    lane = lax.broadcasted_iota(jnp.int32, (1, LANES), 1).astype(jnp.float32)

    def match(g, carry):
        first = (me * table + g * (batch * LANES)).astype(jnp.float32)
        names = [first + (q * LANES) + lane for q in range(batch)]

        def one(r, best):
            best = list(best)
            for i in range(0, rows, 8):
                mark = marks_wide[r, i:i + 8, :]
                prio = prio_wide[r, i:i + 8, :]
                for q in range(batch):
                    best[q] = jnp.maximum(best[q], jnp.where(mark == names[q], prio, 0.0))
            return tuple(best)

        best = lax.fori_loop(0, groups, one, tuple(jnp.zeros((8, LANES), jnp.float32) for _ in range(batch)))
        for q in range(batch):
            top = jnp.max(best[q], axis=0, keepdims=True)
            at = pl.ds(g * batch + q, 1)
            refreshed[at, :] = jnp.where(top > 0.0, top, old[at, :])
        return carry

    lax.fori_loop(0, lines // batch, match, 0)
    subtotal = jnp.sum(jnp.sum(refreshed[...], axis=0, keepdims=True), axis=1, keepdims=True)
    sums[me] = jnp.broadcast_to(subtotal, (1, LANES))
    for j in range(1, groups):
        to_group(sums, sm_send, sm_recv, j).start()

    def drain(t, carry):
        for h in range(2):
            for d in range(1, SIDE):
                ag_copy(t, h, d, spot[h]).wait_send()
                rs_copy(t, h, d).wait_send()

            @pl.when(sec < last)
            def _():
                for d in range(SIDE):
                    line_copy(t, h, d).wait_send()

            @pl.when((sec == last) & (spot[1 - h] != home_of(t)))
            def _():
                last_copy(t, h).wait_send()
        return carry

    lax.fori_loop(0, MICRO, drain, 0)

    @pl.when(sec == 0)
    def _():
        for k in range(rounds):
            for h in range(2):
                for d in range(1, SIDE):
                    in_copy(k, h, d).wait_send()

    @pl.when(sec == last)
    def _():
        for j in range(1, sections):
            up_copy(j).wait_send()

    for j in range(1, groups):
        to_group(marks, mk_send, mk_recv, j).wait_send()
        to_group(result, rw_send, rw_recv, j).wait_send()

    for j in range(1, groups):
        from_group(sums, sm_send, sm_recv, j).wait_recv()
    total = sums[0]
    for r in range(1, groups):
        total = total + sums[r]
    tall = lines // sections
    weights_out[...] = refreshed[pl.ds(sec * tall, tall), :] * (table * groups / total)
    for j in range(1, groups):
        to_group(sums, sm_send, sm_recv, j).wait_send()


def handed(rewards, weights, rewards_out, weights_out):
    rewards_out[...] = rewards[...]
    weights_out[...] = weights[...]


def on_device(
    features, ages, age_table, returns, owners, slots, norm_gain,
    w_gate, w_up, w_down, final_gain, reward_head, old_priority,
):
    sections, groups = lax.axis_size("section"), lax.axis_size("rows")
    rows, width = features.shape
    block = rows * groups // (MICRO * 2 * SIDE)
    rounds = MICRO // SIDE
    ff = w_gate.shape[2]
    even = ff // 256 * 256
    table = old_priority.shape[0]
    lines = table // LANES
    vmem = pl.BlockSpec(memory_space=pltpu.VMEM)
    far = pl.BlockSpec(memory_space=pl.ANY)
    bf16, f32, dma = jnp.bfloat16, jnp.float32, pltpu.SemaphoreType.DMA
    rewards, weights = pl.pallas_call(
        functools.partial(kernel, sections, groups),
        out_shape=(
            jax.ShapeDtypeStruct((1, rows // sections), f32),
            jax.ShapeDtypeStruct((lines // sections, LANES), f32),
        ),
        in_specs=[vmem] * 7 + [far] * 3 + [vmem] * 3,
        out_specs=(vmem, vmem),
        scratch_shapes=[
            pltpu.VMEM((ff, width), bf16),
            pltpu.VMEM((ff, width), bf16),
            pltpu.VMEM((ff, width), bf16),
            pltpu.VMEM((width, 2 * even + 256), bf16),
            pltpu.VMEM((MICRO, 2, block, width), bf16),
            pltpu.VMEM((MICRO, 2, SIDE, block, width), bf16),
            pltpu.VMEM((2 * SIDE * block, ff), bf16),
            pltpu.VMEM((MICRO, 2, SIDE, block, width), bf16),
            pltpu.VMEM((MICRO, 2, SIDE - 1, block, width), bf16),
            pltpu.VMEM((MICRO, 2, block, width), bf16),
            pltpu.VMEM((MICRO, 2, SIDE, block, width), bf16),
            pltpu.VMEM((rounds, 2, SIDE - 1, block, width), bf16),
            pltpu.VMEM((2, width), f32),
            pltpu.VMEM((2, rounds, block, LANES), f32),
            pltpu.VMEM((groups, 1, rows), f32),
            pltpu.VMEM((groups, rows, LANES), f32),
            pltpu.VMEM((groups, 2, rows), f32),
            pltpu.VMEM((groups, rows, LANES), f32),
            pltpu.VMEM((lines, LANES), f32),
            pltpu.VMEM((groups, 1, LANES), f32),
            dma((3,)),
            dma((rounds, 2, SIDE - 1)),
            dma((MICRO, 2, SIDE - 1)), dma((MICRO, 2, SIDE - 1)),
            dma((MICRO, 2, SIDE - 1)), dma((MICRO, 2, SIDE - 1)),
            dma((MICRO, 2, SIDE)), dma((MICRO, 2, SIDE)),
            dma((rounds, 2, SIDE - 1)),
            dma((groups,)), dma((groups,)),
            dma((sections - 1,)), dma((1,)),
            dma((groups,)), dma((groups,)),
            dma((groups,)), dma((groups,)),
        ],
        compiler_params=pltpu.CompilerParams(
            collective_id=0, has_side_effects=True, vmem_limit_bytes=56 * 1024 * 1024
        ),
        name="refresh",
    )(
        features, ages.reshape(1, rows), age_table, returns.reshape(1, rows),
        owners.reshape(1, rows), slots.reshape(1, rows),
        norm_gain, w_gate[0].T, w_up[0].T, w_down[0],
        final_gain.reshape(-1, LANES), reward_head.reshape(-1, LANES),
        old_priority.reshape(lines, LANES),
    )
    rewards, weights = pl.pallas_call(
        handed, out_shape=tuple(jax.ShapeDtypeStruct(each.shape, f32) for each in (rewards, weights)),
        in_specs=[vmem, vmem], out_specs=(vmem, vmem), name="handed",
    )(rewards, weights)
    return rewards.reshape(-1), weights.reshape(-1)


def solution(mesh):
    placed = (
        P("rows", None),
        P("rows"),
        P(),
        P("rows"),
        P("rows", None),
        P("rows"),
        P("section", None),
        P("section", None, "rows"),
        P("section", None, "rows"),
        P("section", "rows", None),
        P(),
        P(),
        P("rows"),
    )
    return jax.shard_map(
        on_device,
        mesh=mesh,
        in_specs=placed,
        out_specs=(P(("rows", "section")), P(("rows", "section"))),
        check_vma=False,
    )
```

time: 617 us -> 283 us (0.46)
  Pallas kernels: 615 us -> 281 us
    pallas_call x1, Pallas kernels: 614 us -> 280 us  [on_device(): pl.pallas_call(functools.partial(kernel, sections, groups), out_shape=(ja...]
where the time goes in v1:
time: 283 us; the launch traced here: 282 us
  Pallas kernels  281 us (99%)
    pallas_call x1, Pallas kernels, on_device(): pl.pallas_call(functools.partial(kernel, sections, groups), out_shape=(ja...  280 us

profile of v1, /device:TPU:1, one launch (start us, length us, event | category | flops | bytes accessed | tf_op | source)
XLA Modules:
  0.0 282.0 jit_solution(1687742622731626844)
XLA Ops:
  0.6 280.1 %refresh.1 = (f32[1,16]{1,0:T(1,128)}, f32[4,128]{1,0:T(4,128)}) custom-call(bf16[128,1536]{1,0:T(8,128)(2,1)} %features.1, s32[1,128]{1,0:T(1,128)} %bitcast.22, bf16[16,1536]{1,0:T(8,128)(2,1)} %age_table.1, f32[1,128]{1,0:T(1,128)} %bitcast.23, s32[1,128]{1,0:T(1,128)} %bitcast.24, s32[1,128]{1,0:T(1,128)} %bitcast.25, f32[1,1536]{1,0:T(1,128)} %gain.1, ...), custom_call_target="tpu_custom_call" | custom-call | tf_op jit(solution)/shard_map/refresh/pallas_call | solution.py:412
  280.8 1.3 handed.1

commit v2 on v1

--- a/solution.py
+++ b/solution.py
@@ -7,7 +7,10 @@
 from jax.experimental.pallas import tpu as pltpu
 from jax.sharding import PartitionSpec as P
 
-MICRO = 16
+MICRO = 32
+ENTER_AHEAD = 3
+WORK_AHEAD = 2
+RING = 8
 SIDE = 4
 MESH = pl.DeviceIdType.MESH
 LANES = 128
@@ -30,7 +33,7 @@
     final_gain, head, old,
     rewards_out, weights_out,
     wg, wu, wd, w_both, state, gathered, hidden, part, part_in, line_out, line_in, last_in,
-    final_row, reward_cols, marks, marks_wide, result, prio_wide, refreshed, sums,
+    final_row, reward_cols, marks, marks_wide, result, prio_wide, tops, shares, spare, sums,
     w_sem,
     in_send, ag_send, ag_recv, rs_send, rs_recv, ln_send, ln_recv, fn_recv,
     mk_send, mk_recv, up_send, up_recv, rw_send, rw_recv, sm_send, sm_recv,
@@ -94,49 +97,52 @@
                 for k in range(rounds):
                     state[k * SIDE + spot[1 - h], h, :, at:at + size] = entry[h, k]
 
+    def turned(load, flat, first):
+        load.wait()
+        for at in range(0, even, 256):
+            w_both[:, first * even + at:first * even + at + 256] = jnp.transpose(flat[at:at + 256, :])
+        w_both[:, 2 * even + first * LANES:2 * even + first * LANES + rest] = jnp.transpose(flat[even:ff, :])
+
+    w_both[:, 2 * even:2 * even + 256] = jnp.zeros((width, 256), jnp.bfloat16)
+    turned(loads[0], wg, 0)
+    turned(loads[1], wu, 1)
+    loads[2].wait()
+
     pl.semaphore_wait(barrier, groups - 1 + sections - 1 + 2 * (SIDE - 1))
 
+    here = {"rows": lax.rem(me + 1, groups)}
+
+    def arrived(ref, recv):
+        remote(ref, ref, in_send.at[0], recv, here).wait_recv()
+
+    def departed(ref, send):
+        remote(ref, ref, send, ln_recv.at[0, 0], here).wait_send()
+
     def to_group(ref, send, recv, j):
-        return remote(ref.at[me], ref.at[me], send.at[j], recv.at[j], {"rows": lax.rem(me + j, groups)})
-
-    def from_group(ref, send, recv, j):
-        spot_ref = ref.at[lax.rem(me + groups - j, groups)]
-        return remote(spot_ref, spot_ref, send.at[j], recv.at[j], {"rows": lax.rem(me + j, groups)})
+        return remote(ref.at[me], ref.at[me], send.at[0], recv.at[0], {"rows": lax.rem(me + j, groups)})
+
+    def all_but_one(ref):
+        return ref.at[pl.ds(0, groups - 1)]
 
     def in_copy(k, h, d):
         t = k * SIDE + spot[1 - h]
         ref = state.at[t, h]
-        return remote(
-            ref, ref, in_send.at[k, h, d - 1], ln_recv.at[t, h, 0], {"rows": on_line(1 - h, step_on(1 - h, d))}
-        )
-
-    def in_from(t, h):
-        ref = state.at[t, h]
-        return remote(ref, ref, in_send.at[0, h, 0], ln_recv.at[t, h, 0], {"rows": on_line(1 - h, step_on(1 - h, 1))})
-
-    def ag_copy(t, h, d, shard):
-        ref = gathered.at[t, h, shard]
-        return remote(
-            ref, ref, ag_send.at[t, h, d - 1], ag_recv.at[t, h, d - 1], {"rows": on_line(h, step_on(h, d))}
-        )
+        return remote(ref, ref, in_send.at[0], ln_recv.at[t, h], {"rows": on_line(1 - h, step_on(1 - h, d))})
+
+    def ag_copy(t, h, d):
+        ref = gathered.at[t, h, spot[h]]
+        return remote(ref, ref, ag_send.at[0], ag_recv.at[lax.rem(t, RING), h], {"rows": on_line(h, step_on(h, d))})
 
     def rs_copy(t, h, d):
         return remote(
-            part.at[t, h, step_on(h, d)], part_in.at[t, h, d - 1], rs_send.at[t, h, d - 1], rs_recv.at[t, h, d - 1],
+            part.at[t, h, step_on(h, d)], part_in.at[t, h, d - 1], rs_send.at[0], rs_recv.at[lax.rem(t, RING), h],
             {"rows": on_line(h, step_on(h, d))},
         )
 
     def line_copy(t, h, d):
-        own = spot[1 - h]
         return remote(
-            line_out.at[t, h], line_in.at[t, h, own], ln_send.at[t, h, d], ln_recv.at[t, h, own],
+            line_out.at[t, h], line_in.at[t, h, spot[1 - h]], ln_send.at[0], ln_recv.at[t, h],
             {"section": jnp.minimum(sec + 1, last), "rows": on_line(1 - h, step_on(1 - h, d))},
-        )
-
-    def line_from(t, h, i):
-        return remote(
-            line_out.at[t, h], line_in.at[t, h, i], ln_send.at[t, h, 0], ln_recv.at[t, h, i],
-            {"section": jnp.maximum(sec - 1, 0)},
         )
 
     def home_of(t):
@@ -147,20 +153,15 @@
         d = lax.rem(home + SIDE - spot[1 - h] + SIDE - 1, SIDE)
         k = t // SIDE
         return remote(
-            line_out.at[t, h], last_in.at[k, h, d], ln_send.at[t, h, 0], fn_recv.at[k, h, d],
+            line_out.at[t, h], last_in.at[k, h, d], ln_send.at[0], fn_recv.at[k, h],
             {"rows": on_line(1 - h, home)},
         )
-
-    def last_from(k, h, d):
-        ref = last_in.at[k, h, d - 1]
-        return remote(ref, ref, ln_send.at[0, h, 0], fn_recv.at[k, h, d - 1], {"rows": on_line(1 - h, step_on(1 - h, d))})
 
     def enter(t):
         for h in range(2):
             @pl.when(sec > 0)
             def _():
-                for i in range(SIDE):
-                    line_from(t, h, i).wait_recv()
+                arrived(line_in.at[t, h], ln_recv.at[t, h])
                 total = line_in[t, h, 0].astype(jnp.float32)
                 for i in range(1, SIDE):
                     total = total + line_in[t, h, i].astype(jnp.float32)
@@ -168,18 +169,17 @@
 
             @pl.when((sec == 0) & (spot[1 - h] != home_of(t)))
             def _():
-                in_from(t, h).wait_recv()
+                arrived(state.at[t, h], ln_recv.at[t, h])
 
             wide = state[t, h].astype(jnp.float32)
             scale = lax.rsqrt(jnp.mean(wide * wide, axis=-1, keepdims=True) + 1e-06)
             gathered[t, h, spot[h]] = (wide * scale * gain[...]).astype(jnp.bfloat16)
             for d in (2, 1, 3):
-                ag_copy(t, h, d, spot[h]).start()
+                ag_copy(t, h, d).start()
 
     def work(t):
         for h in range(2):
-            for d in (1, 3, 2):
-                ag_copy(t, h, d, step_on(h, SIDE - d)).wait_recv()
+            arrived(gathered.at[t, h, pl.ds(0, SIDE - 1)], ag_recv.at[lax.rem(t, RING), h])
         piece = gathered[t].reshape(2 * SIDE * block, width)
         for at in range(0, even, 256):
             gate = jnp.dot(piece, w_both[:, at:at + 256], preferred_element_type=jnp.float32)
@@ -201,8 +201,8 @@
         for h in range(2):
             total = part[t, h, spot[h]].astype(jnp.float32)
             total = total + jnp.where(spot[1 - h] == home, state[t, h].astype(jnp.float32), 0.0)
+            arrived(part_in.at[t, h], rs_recv.at[lax.rem(t, RING), h])
             for d in range(1, SIDE):
-                rs_copy(t, h, d).wait_recv()
                 total = total + part_in[t, h, d - 1].astype(jnp.float32)
             line_out[t, h] = total.astype(jnp.bfloat16)
 
@@ -221,8 +221,8 @@
             @pl.when(spot[1 - h] == home_of(t))
             def _():
                 total = line_out[t, h].astype(jnp.float32)
+                arrived(last_in.at[k, h], fn_recv.at[k, h])
                 for d in range(1, SIDE):
-                    last_from(k, h, d).wait_recv()
                     total = total + last_in[k, h, d - 1].astype(jnp.float32)
                 wide = total.astype(jnp.bfloat16).astype(jnp.float32)
                 scale = lax.rsqrt(jnp.mean(wide * wide, axis=-1, keepdims=True) + 1e-06)
@@ -236,54 +236,92 @@
                 for d in (2, 1, 3):
                     in_copy(k, h, d).start()
 
-    def turned(load, flat, first):
-        load.wait()
-        for at in range(0, even, 256):
-            w_both[:, first * even + at:first * even + at + 256] = jnp.transpose(flat[at:at + 256, :])
-        w_both[:, 2 * even + first * LANES:2 * even + first * LANES + rest] = jnp.transpose(flat[even:ff, :])
-
-    w_both[:, 2 * even:2 * even + 256] = jnp.zeros((width, 256), jnp.bfloat16)
-    turned(loads[0], wg, 0)
     for j in range(1, groups):
         to_group(marks, mk_send, mk_recv, j).start()
 
-    @pl.when(sec == 0)
-    def _():
-        enter(0)
-
-    turned(loads[1], wu, 1)
-    loads[2].wait()
-
-    @pl.when(sec > 0)
-    def _():
-        enter(0)
-
-    def step(t, carry):
-        work(t)
-
-        @pl.when(t + 1 < MICRO)
+    lines = old.shape[0]
+    table = lines * LANES
+    tall = lines // sections
+    batch = 4
+    lane = lax.broadcasted_iota(jnp.int32, (1, LANES), 1).astype(jnp.float32)
+
+    def over_rows(names, join):
+        def one(r, best):
+            best = list(best)
+            for i in range(0, rows, 8):
+                mark = marks_wide[r, i:i + 8, :]
+                value = prio_wide[r, i:i + 8, :]
+                for q in range(batch):
+                    best[q] = join(best[q], jnp.where(mark == names[q], value, 0.0))
+            return tuple(best)
+
+        return lax.fori_loop(0, groups, one, tuple(jnp.zeros((8, LANES), jnp.float32) for _ in range(batch)))
+
+    def count():
+        arrived(all_but_one(marks), mk_recv.at[0])
+        for r in range(groups):
+            marks_wide[r] = jnp.transpose(jnp.broadcast_to(marks[r], (LANES, rows)))
+            prio_wide[r] = jnp.ones((rows, LANES), jnp.float32)
+
+        def by_row(g, carry):
+            found = over_rows([marks[g * batch + q] for q in range(batch)], jnp.add)
+            for q in range(batch):
+                shares[g * batch + q] = 1.0 / jnp.sum(found[q], axis=0, keepdims=True)
+            return carry
+
+        lax.fori_loop(0, groups // batch, by_row, 0)
+
+        def by_entry(g, carry):
+            first = (me * table + g * (batch * LANES)).astype(jnp.float32)
+            found = over_rows([first + (q * LANES) + lane for q in range(batch)], jnp.add)
+            for q in range(batch):
+                at = pl.ds(g * batch + q, 1)
+                spare[at, :] = jnp.where(jnp.sum(found[q], axis=0, keepdims=True) > 0.0, 0.0, old[at, :])
+            return carry
+
+        lax.fori_loop(0, lines // batch, by_entry, 0)
+        subtotal = jnp.sum(jnp.sum(spare[...], axis=0, keepdims=True), axis=1, keepdims=True)
+        sums[me] = jnp.broadcast_to(subtotal, (1, LANES))
+        for j in range(1, groups):
+            to_group(sums, sm_send, sm_recv, j).start()
+
+    @pl.when(sec >= sections // 2)
+    def _():
+        count()
+
+    def step(i, carry):
+        t = i - ENTER_AHEAD
+
+        @pl.when((sec == last) & (t >= 2))
         def _():
-            enter(t + 1)
-
-        @pl.when((sec == last) & (t > 0))
+            finish(t - 2)
+
+        @pl.when(t >= 0)
         def _():
-            finish(t - 1)
-
-        leave(t)
+            leave(t)
+
+        @pl.when(i < MICRO)
+        def _():
+            enter(i)
+
+        @pl.when((t + WORK_AHEAD >= 0) & (t + WORK_AHEAD < MICRO))
+        def _():
+            work(t + WORK_AHEAD)
+
         return carry
 
-    lax.fori_loop(0, MICRO, step, 0)
-
-    for j in range(1, groups):
-        from_group(marks, mk_send, mk_recv, j).wait_recv()
-    for r in range(groups):
-        marks_wide[r] = jnp.transpose(jnp.broadcast_to(marks[r], (LANES, rows)))
+    lax.fori_loop(0, MICRO + ENTER_AHEAD, step, 0)
+
+    @pl.when(sec < sections // 2)
+    def _():
+        count()
 
     def up_copy(j):
-        return remote(result.at[me], result.at[me], up_send.at[j - 1], up_recv.at[0], {"section": last - j})
+        return remote(result.at[me], result.at[me], up_send.at[0], up_recv.at[0], {"section": last - j})
 
     @pl.when(sec == last)
     def _():
+        finish(MICRO - 2)
         finish(MICRO - 1)
         square = reward_cols[...].reshape(rows, LANES)
         on_diagonal = lax.broadcasted_iota(jnp.int32, (rows, rows), 0) == lax.broadcasted_iota(jnp.int32, (rows, rows), 1)
@@ -294,12 +332,31 @@
         for j in range(1, sections):
             up_copy(j).start()
 
+    departed(part_in, ag_send.at[0])
+    departed(part_in, rs_send.at[0])
+    departed(all_but_one(marks), mk_send.at[0])
+
+    @pl.when(sec == 0)
+    def _():
+        departed(part_in.at[pl.ds(0, rounds)], in_send.at[0])
+
+    arrived(all_but_one(sums), sm_recv.at[0])
+    departed(all_but_one(sums), sm_send.at[0])
+    kept = sums[0]
+    for r in range(1, groups):
+        kept = kept + sums[r]
+
     @pl.when(sec < last)
     def _():
-        up_copy(1).wait_recv()
+        departed(line_in, ln_send.at[0])
+        arrived(result.at[me], up_recv.at[0])
 
     for j in range(1, groups):
         to_group(result, rw_send, rw_recv, j).start()
+
+    @pl.when(sec == last)
+    def _():
+        departed(part_in.at[pl.ds(0, rounds)], ln_send.at[0])
 
     mine = result[me, 0:1]
     share = rows // sections
@@ -308,85 +365,30 @@
         picked = jnp.where(sec == s, mine[:, s * share:(s + 1) * share], picked)
     rewards_out[...] = picked
 
-    for j in range(1, groups):
-        from_group(result, rw_send, rw_recv, j).wait_recv()
+    arrived(all_but_one(result), rw_recv.at[0])
     for r in range(groups):
         prio_wide[r] = jnp.transpose(jnp.broadcast_to(result[r, 1:2], (LANES, rows)))
 
-    lines = old.shape[0]
-    table = lines * LANES
-    batch = 4
-    lane = lax.broadcasted_iota(jnp.int32, (1, LANES), 1).astype(jnp.float32)
-
-    def match(g, carry):
-        first = (me * table + g * (batch * LANES)).astype(jnp.float32)
-        names = [first + (q * LANES) + lane for q in range(batch)]
-
-        def one(r, best):
-            best = list(best)
-            for i in range(0, rows, 8):
-                mark = marks_wide[r, i:i + 8, :]
-                prio = prio_wide[r, i:i + 8, :]
-                for q in range(batch):
-                    best[q] = jnp.maximum(best[q], jnp.where(mark == names[q], prio, 0.0))
-            return tuple(best)
-
-        best = lax.fori_loop(0, groups, one, tuple(jnp.zeros((8, LANES), jnp.float32) for _ in range(batch)))
+    def by_row(g, carry):
+        found = over_rows([marks[g * batch + q] for q in range(batch)], jnp.maximum)
         for q in range(batch):
-            top = jnp.max(best[q], axis=0, keepdims=True)
-            at = pl.ds(g * batch + q, 1)
-            refreshed[at, :] = jnp.where(top > 0.0, top, old[at, :])
+            tops[g * batch + q] = jnp.max(found[q], axis=0, keepdims=True) * shares[g * batch + q]
         return carry
 
-    lax.fori_loop(0, lines // batch, match, 0)
-    subtotal = jnp.sum(jnp.sum(refreshed[...], axis=0, keepdims=True), axis=1, keepdims=True)
-    sums[me] = jnp.broadcast_to(subtotal, (1, LANES))
-    for j in range(1, groups):
-        to_group(sums, sm_send, sm_recv, j).start()
-
-    def drain(t, carry):
-        for h in range(2):
-            for d in range(1, SIDE):
-                ag_copy(t, h, d, spot[h]).wait_send()
-                rs_copy(t, h, d).wait_send()
-
-            @pl.when(sec < last)
-            def _():
-                for d in range(SIDE):
-                    line_copy(t, h, d).wait_send()
-
-            @pl.when((sec == last) & (spot[1 - h] != home_of(t)))
-            def _():
-                last_copy(t, h).wait_send()
-        return carry
-
-    lax.fori_loop(0, MICRO, drain, 0)
-
-    @pl.when(sec == 0)
-    def _():
-        for k in range(rounds):
-            for h in range(2):
-                for d in range(1, SIDE):
-                    in_copy(k, h, d).wait_send()
+    lax.fori_loop(0, groups // batch, by_row, 0)
+    named = jnp.sum(jnp.sum(tops[...], axis=0), axis=1, keepdims=True)
+    scale = table * groups / (kept + named)
+    first = (me * table + sec * (tall * LANES)).astype(jnp.float32)
+    found = over_rows([first + (q * LANES) + lane for q in range(batch)], jnp.maximum)
+    for q in range(batch):
+        top = jnp.max(found[q], axis=0, keepdims=True)
+        weights_out[q:q + 1, :] = jnp.where(top > 0.0, top, old[pl.ds(sec * tall + q, 1), :]) * scale
+
+    departed(all_but_one(result), rw_send.at[0])
 
     @pl.when(sec == last)
     def _():
-        for j in range(1, sections):
-            up_copy(j).wait_send()
-
-    for j in range(1, groups):
-        to_group(marks, mk_send, mk_recv, j).wait_send()
-        to_group(result, rw_send, rw_recv, j).wait_send()
-
-    for j in range(1, groups):
-        from_group(sums, sm_send, sm_recv, j).wait_recv()
-    total = sums[0]
-    for r in range(1, groups):
-        total = total + sums[r]
-    tall = lines // sections
-    weights_out[...] = refreshed[pl.ds(sec * tall, tall), :] * (table * groups / total)
-    for j in range(1, groups):
-        to_group(sums, sm_send, sm_recv, j).wait_send()
+        departed(result.at[pl.ds(0, sections - 1)], up_send.at[0])
 
 
 def handed(rewards, weights, rewards_out, weights_out):
@@ -436,18 +438,20 @@
             pltpu.VMEM((groups, rows, LANES), f32),
             pltpu.VMEM((groups, 2, rows), f32),
             pltpu.VMEM((groups, rows, LANES), f32),
+            pltpu.VMEM((groups, 1, LANES), f32),
+            pltpu.VMEM((groups, 1, LANES), f32),
             pltpu.VMEM((lines, LANES), f32),
             pltpu.VMEM((groups, 1, LANES), f32),
             dma((3,)),
-            dma((rounds, 2, SIDE - 1)),
-            dma((MICRO, 2, SIDE - 1)), dma((MICRO, 2, SIDE - 1)),
-            dma((MICRO, 2, SIDE - 1)), dma((MICRO, 2, SIDE - 1)),
-            dma((MICRO, 2, SIDE)), dma((MICRO, 2, SIDE)),
-            dma((rounds, 2, SIDE - 1)),
-            dma((groups,)), dma((groups,)),
-            dma((sections - 1,)), dma((1,)),
-            dma((groups,)), dma((groups,)),
-            dma((groups,)), dma((groups,)),
+            dma((1,)),
+            dma((1,)), dma((RING, 2)),
+            dma((1,)), dma((RING, 2)),
+            dma((1,)), dma((MICRO, 2)),
+            dma((rounds, 2)),
+            dma((1,)), dma((1,)),
+            dma((1,)), dma((1,)),
+            dma((1,)), dma((1,)),
+            dma((1,)), dma((1,)),
         ],
         compiler_params=pltpu.CompilerParams(
             collective_id=0, has_side_effects=True, vmem_limit_bytes=56 * 1024 * 1024

time: 283 us -> 237 us (0.84)
  Pallas kernels: 281 us -> 236 us
    pallas_call x1, Pallas kernels: 280 us -> 235 us  [on_device(): pl.pallas_call(functools.partial(kernel, sections, groups), out_shape=(ja...]
where the time goes in v2:
time: 237 us
  Pallas kernels  236 us (100%)
    pallas_call x1, Pallas kernels, on_device(): pl.pallas_call(functools.partial(kernel, sections, groups), out_shape=(ja...  235 us

profile of v2, /device:TPU:1, one launch (start us, length us, event | category | flops | bytes accessed | tf_op | source)
XLA Modules:
  0.0 236.5 jit_solution(16033743213297214657)
XLA Ops:
  0.6 234.6 %refresh.1 = (f32[1,16]{1,0:T(1,128)}, f32[4,128]{1,0:T(4,128)}) custom-call(bf16[128,1536]{1,0:T(8,128)(2,1)} %features.1, s32[1,128]{1,0:T(1,128)} %bitcast.22, bf16[16,1536]{1,0:T(8,128)(2,1)} %age_table.1, f32[1,128]{1,0:T(1,128)} %bitcast.23, s32[1,128]{1,0:T(1,128)} %bitcast.24, s32[1,128]{1,0:T(1,128)} %bitcast.25, f32[1,1536]{1,0:T(1,128)} %gain.1, ...), custom_call_target="tpu_custom_call" | custom-call | tf_op jit(solution)/shard_map/refresh/pallas_call | solution.py:414
  235.3 1.3 handed.1

commit v3 on v2

--- a/solution.py
+++ b/solution.py
@@ -10,7 +10,7 @@
 MICRO = 32
 ENTER_AHEAD = 3
 WORK_AHEAD = 2
-RING = 8
+RING = 4
 SIDE = 4
 MESH = pl.DeviceIdType.MESH
 LANES = 128
@@ -148,14 +148,18 @@
     def home_of(t):
         return lax.rem(t, SIDE)
 
-    def last_copy(t, h):
+    def last_copy(t, h, k):
         home = home_of(t)
-        d = lax.rem(home + SIDE - spot[1 - h] + SIDE - 1, SIDE)
-        k = t // SIDE
+        where = home * SIDE + k if h == 0 else k * SIDE + home
+        slot = lax.rem(me - where + groups + groups - 1, groups)
         return remote(
-            line_out.at[t, h], last_in.at[k, h, d], ln_send.at[0], fn_recv.at[k, h],
-            {"rows": on_line(1 - h, home)},
+            part.at[t, h, k], last_in.at[t // SIDE, h, slot], rs_send.at[0], fn_recv.at[t // SIDE, h], {"rows": where}
         )
+
+    def normed(t, h):
+        wide = state[t, h].astype(jnp.float32)
+        scale = lax.rsqrt(jnp.mean(wide * wide, axis=-1, keepdims=True) + 1e-06)
+        gathered[t, h, spot[h]] = (wide * scale * gain[...]).astype(jnp.bfloat16)
 
     def enter(t):
         for h in range(2):
@@ -171,15 +175,21 @@
             def _():
                 arrived(state.at[t, h], ln_recv.at[t, h])
 
-            wide = state[t, h].astype(jnp.float32)
-            scale = lax.rsqrt(jnp.mean(wide * wide, axis=-1, keepdims=True) + 1e-06)
-            gathered[t, h, spot[h]] = (wide * scale * gain[...]).astype(jnp.bfloat16)
+            normed(t, h)
             for d in (2, 1, 3):
                 ag_copy(t, h, d).start()
 
     def work(t):
         for h in range(2):
-            arrived(gathered.at[t, h, pl.ds(0, SIDE - 1)], ag_recv.at[lax.rem(t, RING), h])
+            foreign = (sec == 0) & (t == 0) & (spot[1 - h] > 0)
+
+            @pl.when(foreign)
+            def _():
+                arrived(gathered.at[t, h], ag_recv.at[0, h])
+
+            @pl.when(jnp.logical_not(foreign))
+            def _():
+                arrived(gathered.at[t, h, pl.ds(0, SIDE - 1)], ag_recv.at[lax.rem(t, RING), h])
         piece = gathered[t].reshape(2 * SIDE * block, width)
         for at in range(0, even, 256):
             gate = jnp.dot(piece, w_both[:, at:at + 256], preferred_element_type=jnp.float32)
@@ -192,9 +202,20 @@
         for at, size in chunks(width, 256):
             down = jnp.dot(units, wd[:, at:at + size], preferred_element_type=jnp.float32)
             part[t, :, :, :, at:at + size] = down.astype(jnp.bfloat16).reshape(2, SIDE, block, size)
-        for h in range(2):
-            for d in (2, 1, 3):
-                rs_copy(t, h, d).start()
+
+        @pl.when(sec < last)
+        def _():
+            for h in range(2):
+                for d in (2, 1, 3):
+                    rs_copy(t, h, d).start()
+
+        @pl.when(sec == last)
+        def _():
+            for h in range(2):
+                for k in range(SIDE):
+                    @pl.when((spot[h] != k) | (spot[1 - h] != home_of(t)))
+                    def _():
+                        last_copy(t, h, k).start()
 
     def leave(t):
         home = home_of(t)
@@ -206,24 +227,18 @@
                 total = total + part_in[t, h, d - 1].astype(jnp.float32)
             line_out[t, h] = total.astype(jnp.bfloat16)
 
-            @pl.when(sec < last)
-            def _():
-                for d in (2, 1, 3, 0):
-                    line_copy(t, h, d).start()
-
-            @pl.when((sec == last) & (spot[1 - h] != home))
-            def _():
-                last_copy(t, h).start()
+            for d in (0, 2, 1, 3):
+                line_copy(t, h, d).start()
 
     def finish(t):
         k = t // SIDE
         for h in range(2):
             @pl.when(spot[1 - h] == home_of(t))
             def _():
-                total = line_out[t, h].astype(jnp.float32)
+                total = state[t, h].astype(jnp.float32) + part[t, h, spot[h]].astype(jnp.float32)
                 arrived(last_in.at[k, h], fn_recv.at[k, h])
-                for d in range(1, SIDE):
-                    total = total + last_in[k, h, d - 1].astype(jnp.float32)
+                for j in range(groups - 1):
+                    total = total + last_in[k, h, j].astype(jnp.float32)
                 wide = total.astype(jnp.bfloat16).astype(jnp.float32)
                 scale = lax.rsqrt(jnp.mean(wide * wide, axis=-1, keepdims=True) + 1e-06)
                 value = jnp.sum(wide * scale * final_row[0:1] * final_row[1:2], axis=-1, keepdims=True)
@@ -231,10 +246,19 @@
 
     @pl.when(sec == 0)
     def _():
+        for h in range(2):
+            @pl.when(spot[1 - h] == 0)
+            def _():
+                normed(0, h)
+                ref = gathered.at[0, h, spot[h]]
+                for j in range(1, groups):
+                    remote(ref, ref, ag_send.at[0], ag_recv.at[0, h], {"rows": lax.rem(me + j, groups)}).start()
         for k in range(rounds):
             for h in range(2):
-                for d in (2, 1, 3):
-                    in_copy(k, h, d).start()
+                @pl.when((spot[1 - h] > 0) | (k > 0))
+                def _():
+                    for d in (2, 1, 3):
+                        in_copy(k, h, d).start()
 
     for j in range(1, groups):
         to_group(marks, mk_send, mk_recv, j).start()
@@ -292,17 +316,17 @@
     def step(i, carry):
         t = i - ENTER_AHEAD
 
-        @pl.when((sec == last) & (t >= 2))
+        @pl.when((sec == last) & (t >= 0))
         def _():
-            finish(t - 2)
-
-        @pl.when(t >= 0)
+            finish(t)
+
+        @pl.when((sec < last) & (t >= 0))
         def _():
             leave(t)
 
-        @pl.when(i < MICRO)
+        @pl.when((i + head_start < MICRO) & ((sec > 0) | (i + head_start > 0)))
         def _():
-            enter(i)
+            enter(i + head_start)
 
         @pl.when((t + WORK_AHEAD >= 0) & (t + WORK_AHEAD < MICRO))
         def _():
@@ -310,6 +334,8 @@
 
         return carry
 
+    head_start = jnp.where(sec == 0, 1, 0)
+
     lax.fori_loop(0, MICRO + ENTER_AHEAD, step, 0)
 
     @pl.when(sec < sections // 2)
@@ -321,8 +347,6 @@
 
     @pl.when(sec == last)
     def _():
-        finish(MICRO - 2)
-        finish(MICRO - 1)
         square = reward_cols[...].reshape(rows, LANES)
         on_diagonal = lax.broadcasted_iota(jnp.int32, (rows, rows), 0) == lax.broadcasted_iota(jnp.int32, (rows, rows), 1)
         row = jnp.sum(jnp.where(on_diagonal, square, 0.0), axis=0, keepdims=True)
@@ -332,13 +356,34 @@
         for j in range(1, sections):
             up_copy(j).start()
 
-    departed(part_in, ag_send.at[0])
-    departed(part_in, rs_send.at[0])
+
+    @pl.when(sec > 0)
+    def _():
+        departed(part_in, ag_send.at[0])
+
+
+    @pl.when(sec < last)
+    def _():
+        departed(part_in, rs_send.at[0])
+
+    @pl.when(sec == last)
+    def _():
+        departed(part.at[pl.ds(0, MICRO - rounds // SIDE)], rs_send.at[0])
+
     departed(all_but_one(marks), mk_send.at[0])
 
     @pl.when(sec == 0)
     def _():
-        departed(part_in.at[pl.ds(0, rounds)], in_send.at[0])
+        departed(part_in.at[pl.ds(0, MICRO - 1)], ag_send.at[0])
+        departed(part_in.at[pl.ds(0, rounds - 1)], in_send.at[0])
+        for h in range(2):
+            @pl.when(spot[1 - h] == 0)
+            def _():
+                departed(last_in.at[0, 0], ag_send.at[0])
+
+            @pl.when(spot[1 - h] > 0)
+            def _():
+                departed(part_in.at[0, 0], in_send.at[0])
 
     arrived(all_but_one(sums), sm_recv.at[0])
     departed(all_but_one(sums), sm_send.at[0])
@@ -353,10 +398,6 @@
 
     for j in range(1, groups):
         to_group(result, rw_send, rw_recv, j).start()
-
-    @pl.when(sec == last)
-    def _():
-        departed(part_in.at[pl.ds(0, rounds)], ln_send.at[0])
 
     mine = result[me, 0:1]
     share = rows // sections
@@ -431,7 +472,7 @@
             pltpu.VMEM((MICRO, 2, SIDE - 1, block, width), bf16),
             pltpu.VMEM((MICRO, 2, block, width), bf16),
             pltpu.VMEM((MICRO, 2, SIDE, block, width), bf16),
-            pltpu.VMEM((rounds, 2, SIDE - 1, block, width), bf16),
+            pltpu.VMEM((rounds, 2, groups - 1, block, width), bf16),
             pltpu.VMEM((2, width), f32),
             pltpu.VMEM((2, rounds, block, LANES), f32),
             pltpu.VMEM((groups, 1, rows), f32),

time: 237 us -> 264 us (1.11)
  Pallas kernels: 236 us -> 263 us
    pallas_call x1, Pallas kernels: 235 us -> 261 us  [on_device(): pl.pallas_call(functools.partial(kernel, sections, groups), out_shape=(ja...]
where the time goes in v3:
time: 264 us; the launch traced here: 263 us
  Pallas kernels  263 us (100%)
    pallas_call x1, Pallas kernels, on_device(): pl.pallas_call(functools.partial(kernel, sections, groups), out_shape=(ja...  261 us

profile of v3, /device:TPU:1, one launch (start us, length us, event | category | flops | bytes accessed | tf_op | source)
XLA Modules:
  0.0 263.3 jit_solution(12249676823492475030)
XLA Ops:
  0.6 261.4 %refresh.1 = (f32[1,16]{1,0:T(1,128)}, f32[4,128]{1,0:T(4,128)}) custom-call(bf16[128,1536]{1,0:T(8,128)(2,1)} %features.1, s32[1,128]{1,0:T(1,128)} %bitcast.22, bf16[16,1536]{1,0:T(8,128)(2,1)} %age_table.1, f32[1,128]{1,0:T(1,128)} %bitcast.23, s32[1,128]{1,0:T(1,128)} %bitcast.24, s32[1,128]{1,0:T(1,128)} %bitcast.25, f32[1,1536]{1,0:T(1,128)} %gain.1, ...), custom_call_target="tpu_custom_call" | custom-call | tf_op jit(solution)/shard_map/refresh/pallas_call | solution.py:455
  262.0 1.3 handed.1

commit v4 on v2

--- a/solution.py
+++ b/solution.py
@@ -10,7 +10,7 @@
 MICRO = 32
 ENTER_AHEAD = 3
 WORK_AHEAD = 2
-RING = 8
+RING = 4
 SIDE = 4
 MESH = pl.DeviceIdType.MESH
 LANES = 128
@@ -157,6 +157,11 @@
             {"rows": on_line(1 - h, home)},
         )
 
+    def normed(t, h):
+        wide = state[t, h].astype(jnp.float32)
+        scale = lax.rsqrt(jnp.mean(wide * wide, axis=-1, keepdims=True) + 1e-06)
+        gathered[t, h, spot[h]] = (wide * scale * gain[...]).astype(jnp.bfloat16)
+
     def enter(t):
         for h in range(2):
             @pl.when(sec > 0)
@@ -171,15 +176,21 @@
             def _():
                 arrived(state.at[t, h], ln_recv.at[t, h])
 
-            wide = state[t, h].astype(jnp.float32)
-            scale = lax.rsqrt(jnp.mean(wide * wide, axis=-1, keepdims=True) + 1e-06)
-            gathered[t, h, spot[h]] = (wide * scale * gain[...]).astype(jnp.bfloat16)
+            normed(t, h)
             for d in (2, 1, 3):
                 ag_copy(t, h, d).start()
 
     def work(t):
         for h in range(2):
-            arrived(gathered.at[t, h, pl.ds(0, SIDE - 1)], ag_recv.at[lax.rem(t, RING), h])
+            foreign = (sec == 0) & (t == 0) & (spot[1 - h] > 0)
+
+            @pl.when(foreign)
+            def _():
+                arrived(gathered.at[t, h], ag_recv.at[0, h])
+
+            @pl.when(jnp.logical_not(foreign))
+            def _():
+                arrived(gathered.at[t, h, pl.ds(0, SIDE - 1)], ag_recv.at[lax.rem(t, RING), h])
         piece = gathered[t].reshape(2 * SIDE * block, width)
         for at in range(0, even, 256):
             gate = jnp.dot(piece, w_both[:, at:at + 256], preferred_element_type=jnp.float32)
@@ -192,8 +203,8 @@
         for at, size in chunks(width, 256):
             down = jnp.dot(units, wd[:, at:at + size], preferred_element_type=jnp.float32)
             part[t, :, :, :, at:at + size] = down.astype(jnp.bfloat16).reshape(2, SIDE, block, size)
-        for h in range(2):
-            for d in (2, 1, 3):
+        for d in (2, 1, 3):
+            for h in range(2):
                 rs_copy(t, h, d).start()
 
     def leave(t):
@@ -208,7 +219,7 @@
 
             @pl.when(sec < last)
             def _():
-                for d in (2, 1, 3, 0):
+                for d in (0, 2, 1, 3):
                     line_copy(t, h, d).start()
 
             @pl.when((sec == last) & (spot[1 - h] != home))
@@ -231,10 +242,19 @@
 
     @pl.when(sec == 0)
     def _():
+        for h in range(2):
+            @pl.when(spot[1 - h] == 0)
+            def _():
+                normed(0, h)
+                ref = gathered.at[0, h, spot[h]]
+                for j in range(1, groups):
+                    remote(ref, ref, ag_send.at[0], ag_recv.at[0, h], {"rows": lax.rem(me + j, groups)}).start()
         for k in range(rounds):
             for h in range(2):
-                for d in (2, 1, 3):
-                    in_copy(k, h, d).start()
+                @pl.when((spot[1 - h] > 0) | (k > 0))
+                def _():
+                    for d in (2, 1, 3):
+                        in_copy(k, h, d).start()
 
     for j in range(1, groups):
         to_group(marks, mk_send, mk_recv, j).start()
@@ -300,15 +320,17 @@
         def _():
             leave(t)
 
-        @pl.when(i < MICRO)
+        @pl.when((i + head_start < MICRO) & ((sec > 0) | (i + head_start > 0)))
         def _():
-            enter(i)
+            enter(i + head_start)
 
         @pl.when((t + WORK_AHEAD >= 0) & (t + WORK_AHEAD < MICRO))
         def _():
             work(t + WORK_AHEAD)
 
         return carry
+
+    head_start = jnp.where(sec == 0, 1, 0)
 
     lax.fori_loop(0, MICRO + ENTER_AHEAD, step, 0)
 
@@ -332,13 +354,26 @@
         for j in range(1, sections):
             up_copy(j).start()
 
-    departed(part_in, ag_send.at[0])
+
+    @pl.when(sec > 0)
+    def _():
+        departed(part_in, ag_send.at[0])
+
     departed(part_in, rs_send.at[0])
     departed(all_but_one(marks), mk_send.at[0])
 
     @pl.when(sec == 0)
     def _():
-        departed(part_in.at[pl.ds(0, rounds)], in_send.at[0])
+        departed(part_in.at[pl.ds(0, MICRO - 1)], ag_send.at[0])
+        departed(part_in.at[pl.ds(0, rounds - 1)], in_send.at[0])
+        for h in range(2):
+            @pl.when(spot[1 - h] == 0)
+            def _():
+                departed(part_in.at[pl.ds(0, 5), 0], ag_send.at[0])
+
+            @pl.when(spot[1 - h] > 0)
+            def _():
+                departed(part_in.at[0, 0], in_send.at[0])
 
     arrived(all_but_one(sums), sm_recv.at[0])
     departed(all_but_one(sums), sm_send.at[0])

time: 237 us -> 235 us (level)
  no operation moved by 1% of the time
where the time goes in v4:
time: 235 us
  Pallas kernels  234 us (100%)
    pallas_call x1, Pallas kernels, on_device(): pl.pallas_call(functools.partial(kernel, sections, groups), out_shape=(ja...  233 us

profile of v4, /device:TPU:1, one launch (start us, length us, event | category | flops | bytes accessed | tf_op | source)
XLA Modules:
  0.0 234.6 jit_solution(18274109788236238566)
XLA Ops:
  0.6 232.7 %refresh.1 = (f32[1,16]{1,0:T(1,128)}, f32[4,128]{1,0:T(4,128)}) custom-call(bf16[128,1536]{1,0:T(8,128)(2,1)} %features.1, s32[1,128]{1,0:T(1,128)} %bitcast.22, bf16[16,1536]{1,0:T(8,128)(2,1)} %age_table.1, f32[1,128]{1,0:T(1,128)} %bitcast.23, s32[1,128]{1,0:T(1,128)} %bitcast.24, s32[1,128]{1,0:T(1,128)} %bitcast.25, f32[1,1536]{1,0:T(1,128)} %gain.1, ...), custom_call_target="tpu_custom_call" | custom-call | tf_op jit(solution)/shard_map/refresh/pallas_call | solution.py:449
  233.4 1.3 handed.1

commit v5 on v4

--- a/solution.py
+++ b/solution.py
@@ -277,8 +277,33 @@
 
         return lax.fori_loop(0, groups, one, tuple(jnp.zeros((8, LANES), jnp.float32) for _ in range(batch)))
 
+    soon = [r for r in range(groups) if max(r % SIDE, r // SIDE) < SIDE - 1]
+    late = [r for r in range(groups) if r not in soon]
+    own_late = (spot[0] == SIDE - 1) | (spot[1] == SIDE - 1)
+
+    def largest(homes, fresh):
+        for r in homes:
+            prio_wide[r] = jnp.transpose(jnp.broadcast_to(result[r, 1:2], (LANES, rows)))
+
+        def by_name(g, carry):
+            names = [marks[g * batch + q] for q in range(batch)]
+            best = [jnp.zeros((8, LANES), jnp.float32) if fresh else tops[g * batch + q] for q in range(batch)]
+            for r in homes:
+                for i in range(0, rows, 8):
+                    mark = marks_wide[r, i:i + 8, :]
+                    value = prio_wide[r, i:i + 8, :]
+                    for q in range(batch):
+                        best[q] = jnp.maximum(best[q], jnp.where(mark == names[q], value, 0.0))
+            for q in range(batch):
+                tops[g * batch + q] = best[q]
+            return carry
+
+        lax.fori_loop(0, (groups + tall) // batch, by_name, 0)
+
     def count():
         arrived(all_but_one(marks), mk_recv.at[0])
+        for q in range(tall):
+            marks[groups + q] = (me * table + (sec * tall + q) * LANES).astype(jnp.float32) + lane
         for r in range(groups):
             marks_wide[r] = jnp.transpose(jnp.broadcast_to(marks[r], (LANES, rows)))
             prio_wide[r] = jnp.ones((rows, LANES), jnp.float32)
@@ -386,8 +411,22 @@
         departed(line_in, ln_send.at[0])
         arrived(result.at[me], up_recv.at[0])
 
-    for j in range(1, groups):
-        to_group(result, rw_send, rw_recv, j).start()
+    def give(kind):
+        for j in range(1, groups):
+            remote(
+                result.at[me], result.at[me], rw_send.at[0], rw_recv.at[kind], {"rows": lax.rem(me + j, groups)}
+            ).start()
+
+    def take(kind, amount):
+        arrived(result.at[pl.ds(0, amount)], rw_recv.at[kind])
+
+    @pl.when(own_late)
+    def _():
+        give(1)
+
+    @pl.when(jnp.logical_not(own_late))
+    def _():
+        give(0)
 
     @pl.when(sec == last)
     def _():
@@ -400,23 +439,31 @@
         picked = jnp.where(sec == s, mine[:, s * share:(s + 1) * share], picked)
     rewards_out[...] = picked
 
-    arrived(all_but_one(result), rw_recv.at[0])
+    @pl.when(own_late)
+    def _():
+        take(0, len(soon))
+
+    @pl.when(jnp.logical_not(own_late))
+    def _():
+        take(0, len(soon) - 1)
+
+    largest(soon, True)
+
+    @pl.when(own_late)
+    def _():
+        take(1, len(late) - 1)
+
+    @pl.when(jnp.logical_not(own_late))
+    def _():
+        take(1, len(late))
+
+    largest(late, False)
+    named = jnp.zeros((1, LANES), jnp.float32)
     for r in range(groups):
-        prio_wide[r] = jnp.transpose(jnp.broadcast_to(result[r, 1:2], (LANES, rows)))
-
-    def by_row(g, carry):
-        found = over_rows([marks[g * batch + q] for q in range(batch)], jnp.maximum)
-        for q in range(batch):
-            tops[g * batch + q] = jnp.max(found[q], axis=0, keepdims=True) * shares[g * batch + q]
-        return carry
-
-    lax.fori_loop(0, groups // batch, by_row, 0)
-    named = jnp.sum(jnp.sum(tops[...], axis=0), axis=1, keepdims=True)
-    scale = table * groups / (kept + named)
-    first = (me * table + sec * (tall * LANES)).astype(jnp.float32)
-    found = over_rows([first + (q * LANES) + lane for q in range(batch)], jnp.maximum)
-    for q in range(batch):
-        top = jnp.max(found[q], axis=0, keepdims=True)
+        named = named + jnp.max(tops[r], axis=0, keepdims=True) * shares[r]
+    scale = table * groups / (kept + jnp.sum(named, axis=1, keepdims=True))
+    for q in range(tall):
+        top = jnp.max(tops[groups + q], axis=0, keepdims=True)
         weights_out[q:q + 1, :] = jnp.where(top > 0.0, top, old[pl.ds(sec * tall + q, 1), :]) * scale
 
     departed(all_but_one(result), rw_send.at[0])
@@ -469,11 +516,11 @@
             pltpu.VMEM((rounds, 2, SIDE - 1, block, width), bf16),
             pltpu.VMEM((2, width), f32),
             pltpu.VMEM((2, rounds, block, LANES), f32),
-            pltpu.VMEM((groups, 1, rows), f32),
+            pltpu.VMEM((groups + lines // sections, 1, rows), f32),
             pltpu.VMEM((groups, rows, LANES), f32),
             pltpu.VMEM((groups, 2, rows), f32),
             pltpu.VMEM((groups, rows, LANES), f32),
-            pltpu.VMEM((groups, 1, LANES), f32),
+            pltpu.VMEM((groups + lines // sections, 8, LANES), f32),
             pltpu.VMEM((groups, 1, LANES), f32),
             pltpu.VMEM((lines, LANES), f32),
             pltpu.VMEM((groups, 1, LANES), f32),
@@ -485,7 +532,7 @@
             dma((rounds, 2)),
             dma((1,)), dma((1,)),
             dma((1,)), dma((1,)),
-            dma((1,)), dma((1,)),
+            dma((1,)), dma((2,)),
             dma((1,)), dma((1,)),
         ],
         compiler_params=pltpu.CompilerParams(

time: 235 us -> 234 us (level)
  no operation moved by 1% of the time
where the time goes in v5:
time: 234 us; the launch traced here: 233 us
  Pallas kernels  233 us (100%)
    pallas_call x1, Pallas kernels, on_device(): pl.pallas_call(functools.partial(kernel, sections, groups), out_shape=(ja...  232 us

profile of v5, /device:TPU:1, one launch (start us, length us, event | category | flops | bytes accessed | tf_op | source)
XLA Modules:
  0.0 233.4 jit_solution(16863429020171341717)
XLA Ops:
  0.6 231.5 %refresh.1 = (f32[1,16]{1,0:T(1,128)}, f32[4,128]{1,0:T(4,128)}) custom-call(bf16[128,1536]{1,0:T(8,128)(2,1)} %features.1, s32[1,128]{1,0:T(1,128)} %bitcast.22, bf16[16,1536]{1,0:T(8,128)(2,1)} %age_table.1, f32[1,128]{1,0:T(1,128)} %bitcast.23, s32[1,128]{1,0:T(1,128)} %bitcast.24, s32[1,128]{1,0:T(1,128)} %bitcast.25, f32[1,1536]{1,0:T(1,128)} %gain.1, ...), custom_call_target="tpu_custom_call" | custom-call | tf_op jit(solution)/shard_map/refresh/pallas_call | solution.py:496
  232.2 1.3 handed.1

commit v6 on v5

--- a/solution.py
+++ b/solution.py
@@ -49,6 +49,11 @@
     last = sections - 1
     rounds = MICRO // SIDE
 
+    far_first = sorted(range(1, groups), key=lambda j: -min(j % SIDE, SIDE - j % SIDE) - min(j // SIDE, SIDE - j // SIDE))
+
+    def across(j):
+        return {"rows": lax.rem(spot[1] + j // SIDE, SIDE) * SIDE + lax.rem(spot[0] + j % SIDE, SIDE)}
+
     def step_on(axis, d):
         return lax.rem(spot[axis] + d, SIDE)
 
@@ -247,8 +252,8 @@
             def _():
                 normed(0, h)
                 ref = gathered.at[0, h, spot[h]]
-                for j in range(1, groups):
-                    remote(ref, ref, ag_send.at[0], ag_recv.at[0, h], {"rows": lax.rem(me + j, groups)}).start()
+                for j in far_first:
+                    remote(ref, ref, ag_send.at[0], ag_recv.at[0, h], across(j)).start()
         for k in range(rounds):
             for h in range(2):
                 @pl.when((spot[1 - h] > 0) | (k > 0))
@@ -376,7 +381,7 @@
         priority = jnp.exp(0.6 * jnp.log(jnp.abs(row - returns[...]) + 0.05))
         result[me, 0:1] = row
         result[me, 1:2] = priority
-        for j in range(1, sections):
+        for j in sorted(range(1, sections), key=lambda j: abs(j - sections // 2)):
             up_copy(j).start()
 
 
@@ -412,10 +417,8 @@
         arrived(result.at[me], up_recv.at[0])
 
     def give(kind):
-        for j in range(1, groups):
-            remote(
-                result.at[me], result.at[me], rw_send.at[0], rw_recv.at[kind], {"rows": lax.rem(me + j, groups)}
-            ).start()
+        for j in far_first:
+            remote(result.at[me], result.at[me], rw_send.at[0], rw_recv.at[kind], across(j)).start()
 
     def take(kind, amount):
         arrived(result.at[pl.ds(0, amount)], rw_recv.at[kind])

time: 234 us -> 235 us (level)
  no operation moved by 1% of the time
where the time goes in v6:
time: 235 us
  Pallas kernels  234 us (100%)
    pallas_call x1, Pallas kernels, on_device(): pl.pallas_call(functools.partial(kernel, sections, groups), out_shape=(ja...  233 us

profile of v6, /device:TPU:1, one launch (start us, length us, event | category | flops | bytes accessed | tf_op | source)
XLA Modules:
  0.0 235.1 jit_solution(883093066492156786)
XLA Ops:
  0.6 233.2 %refresh.1 = (f32[1,16]{1,0:T(1,128)}, f32[4,128]{1,0:T(4,128)}) custom-call(bf16[128,1536]{1,0:T(8,128)(2,1)} %features.1, s32[1,128]{1,0:T(1,128)} %bitcast.22, bf16[16,1536]{1,0:T(8,128)(2,1)} %age_table.1, f32[1,128]{1,0:T(1,128)} %bitcast.23, s32[1,128]{1,0:T(1,128)} %bitcast.24, s32[1,128]{1,0:T(1,128)} %bitcast.25, f32[1,1536]{1,0:T(1,128)} %gain.1, ...), custom_call_target="tpu_custom_call" | custom-call | tf_op jit(solution)/shard_map/refresh/pallas_call | solution.py:499
  233.9 1.3 handed.1
